TPU v7x, 16 devices: a whole 2x2x2 slice. The times are simulated.
16 devices in a mesh: dp: 4 (over z, y), tp: 4 (over x, core).
Axes of the slice: x: 2, y: 2, z: 2, core: 2. Of those that a mesh axis runs over, the one named last changes fastest.
Arguments:
- hidden: bfloat16 [4, 128, 5120], P('dp', 'tp'), parts along dimension 0
- vision: bfloat16 [4, 512, 5120], P('dp', 'tp'), parts along dimension 0
- positions: int32 [4, 128], P('dp', 'tp'), parts along dimension 0
- tile_mask: int32 [4, 128, 4], P('dp', 'tp'), parts along dimension 0
- ln1_a: bfloat16 [5120], replicated
- wq_a: bfloat16 [5120, 5120], P(None, 'tp')
- wk_a: bfloat16 [5120, 1024], P(None, 'tp')
- wv_a: bfloat16 [5120, 1024], P(None, 'tp')
- wo_a: bfloat16 [5120, 5120], P('tp')
- ln2_a: bfloat16 [5120], replicated
- wg_a: bfloat16 [5120, 13824], P(None, 'tp')
- wu_a: bfloat16 [5120, 13824], P(None, 'tp')
- wd_a: bfloat16 [13824, 5120], P('tp')
- ln1_b: bfloat16 [5120], replicated
- wq_b: bfloat16 [5120, 5120], P(None, 'tp')
- q_norm: bfloat16 [128], replicated
- wk_b: bfloat16 [5120, 1024], P(None, 'tp')
- wv_b: bfloat16 [5120, 1024], P(None, 'tp')
- k_norm: bfloat16 [128], replicated
- wo_b: bfloat16 [5120, 5120], P('tp')
- ln2_b: bfloat16 [5120], replicated
- wg_b: bfloat16 [5120, 13824], P(None, 'tp')
- wu_b: bfloat16 [5120, 13824], P(None, 'tp')
- wd_b: bfloat16 [13824, 5120], P('tp')
- xgates: float32 [2], replicated
Outputs:
- output: bfloat16 [4, 128, 5120], P('dp', 'tp'), parts along dimension 0
There are 4 independent parts. A program takes and returns all parts, laid end to end along the dimension named above; an argument that names none is the same for every part.
All inputs are finite; a program needn't handle non-finite values.
Results may differ from a plain program's by a relative error of at most 0.015711.
Values are sent between devices in bfloat16 or wider.
A program may use at most 1.25 GiB of HBM per device.

v0:
```python
import math
import jax
import jax.numpy as jnp
from jax import lax
from jax.sharding import PartitionSpec as P

ROPE_THETA = 500000.0
ROPE_FACTOR = 8.0
LOW_FACTOR = 1.0
HIGH_FACTOR = 4.0
ORIG_CONTEXT = 8192.0
NORM_EPS = 1e-5
MASK_VALUE = -1e30


def rope_table(head_dim):
    low_wave = ORIG_CONTEXT / LOW_FACTOR
    high_wave = ORIG_CONTEXT / HIGH_FACTOR
    freq_list = []
    for freq_idx in range(head_dim // 2):
        base_freq = 1.0 / (ROPE_THETA ** (2.0 * freq_idx / head_dim))
        wave_len = 2.0 * math.pi / base_freq
        if wave_len > low_wave:
            freq_list.append(base_freq / ROPE_FACTOR)
        elif wave_len < high_wave:
            freq_list.append(base_freq)
        else:
            smooth = (ORIG_CONTEXT / wave_len - LOW_FACTOR) / (HIGH_FACTOR - LOW_FACTOR)
            freq_list.append((1.0 - smooth) * base_freq / ROPE_FACTOR + smooth * base_freq)
    return jnp.array(freq_list, dtype=jnp.float32)


def rms_scale(values, norm_gain):
    values = values.astype(jnp.float32)
    mean_sq = jnp.mean(values * values, axis=-1, keepdims=True)
    return values * lax.rsqrt(mean_sq + NORM_EPS) * norm_gain.astype(jnp.float32)


def rotate(values, cos_tab, sin_tab):
    half_dim = values.shape[-1] // 2
    first_half = values[..., :half_dim]
    second_half = values[..., half_dim:]
    return jnp.concatenate([first_half * cos_tab - second_half * sin_tab, second_half * cos_tab + first_half * sin_tab], axis=-1)


def self_attend(queries, key_vecs, val_vecs):
    seq_len = queries.shape[3]
    head_dim = queries.shape[4]
    scores = jnp.einsum('bgrtd,bsgd->bgrts', queries, key_vecs, preferred_element_type=jnp.float32) * (head_dim ** -0.5)
    causal = lax.broadcasted_iota(jnp.int32, (seq_len, seq_len), 0) >= lax.broadcasted_iota(jnp.int32, (seq_len, seq_len), 1)
    weights = jax.nn.softmax(jnp.where(causal, scores, MASK_VALUE), axis=-1).astype(jnp.bfloat16)
    return jnp.einsum('bgrts,bsgd->bgrtd', weights, val_vecs, preferred_element_type=jnp.float32).astype(jnp.bfloat16)


def cross_attend(queries, key_vecs, val_vecs, visible):
    batch_len, kv_groups, rep_heads, seq_len, head_dim = queries.shape
    vis_len = key_vecs.shape[1]
    tile_count = visible.shape[2]
    scores = jnp.einsum('bgrtd,bsgd->bgrts', queries, key_vecs, preferred_element_type=jnp.float32) * (head_dim ** -0.5)
    scores = scores.reshape(batch_len, kv_groups, rep_heads, seq_len, tile_count, vis_len // tile_count)
    scores = jnp.where(visible[:, None, None, :, :, None], scores, MASK_VALUE)
    weights = jax.nn.softmax(scores.reshape(batch_len, kv_groups, rep_heads, seq_len, vis_len), axis=-1).astype(jnp.bfloat16)
    return jnp.einsum('bgrts,bsgd->bgrtd', weights, val_vecs, preferred_element_type=jnp.float32).astype(jnp.bfloat16)


def gather_rows(values):
    return lax.all_gather(values, 'tp', axis=1, tiled=True)


def scatter_sum(partial):
    return lax.psum_scatter(partial, 'tp', scatter_dimension=1, tiled=True).astype(jnp.float32)


def gated_mlp(resid, norm_gain, w_gate, w_up, w_down):
    gathered = gather_rows(rms_scale(resid, norm_gain).astype(jnp.bfloat16))
    gate_proj = jnp.einsum('btd,df->btf', gathered, w_gate, preferred_element_type=jnp.float32)
    up_proj = jnp.einsum('btd,df->btf', gathered, w_up, preferred_element_type=jnp.float32)
    activated = (jax.nn.silu(gate_proj) * up_proj).astype(jnp.bfloat16)
    partial = jnp.einsum('btf,fd->btd', activated, w_down, preferred_element_type=jnp.float32).astype(jnp.bfloat16)
    return scatter_sum(partial)


def solution(mesh):
    act_spec = P('dp', 'tp', None)
    col_spec = P(None, 'tp')
    row_spec = P('tp', None)
    layer_a = (P(), col_spec, col_spec, col_spec, row_spec, P(), col_spec, col_spec, row_spec)
    layer_b = (P(), col_spec, P(), col_spec, col_spec, P(), row_spec, P(), col_spec, col_spec, row_spec, P())
    in_specs = (act_spec, act_spec, P('dp', 'tp'), act_spec) + layer_a + layer_b

    def body(hidden, vision, positions, tile_mask, ln1_a, wq_a, wk_a, wv_a, wo_a, ln2_a, wg_a, wu_a, wd_a, ln1_b, wq_b, q_norm, wk_b, wv_b, k_norm, wo_b, ln2_b, wg_b, wu_b, wd_b, xgates):
        head_dim = q_norm.shape[0]
        model_dim = hidden.shape[2]
        kv_local = wk_a.shape[1] // head_dim
        rep_heads = wq_a.shape[1] // head_dim // kv_local
        query_shape = (model_dim, kv_local, rep_heads, head_dim)
        head_shape = (model_dim, kv_local, head_dim)
        out_shape = (kv_local, rep_heads, head_dim, model_dim)
        angles = gather_rows(positions).astype(jnp.float32)[..., None] * rope_table(head_dim)
        cos_tab = jnp.cos(angles)
        sin_tab = jnp.sin(angles)
        gathered = gather_rows(rms_scale(hidden, ln1_a).astype(jnp.bfloat16))
        queries = jnp.einsum('btd,dgre->bgrte', gathered, wq_a.reshape(query_shape), preferred_element_type=jnp.float32)
        queries = rotate(queries, cos_tab[:, None, None], sin_tab[:, None, None]).astype(jnp.bfloat16)
        key_vecs = jnp.einsum('btd,dge->btge', gathered, wk_a.reshape(head_shape), preferred_element_type=jnp.float32)
        key_vecs = rotate(key_vecs, cos_tab[:, :, None], sin_tab[:, :, None]).astype(jnp.bfloat16)
        val_vecs = jnp.einsum('btd,dge->btge', gathered, wv_a.reshape(head_shape), preferred_element_type=jnp.float32).astype(jnp.bfloat16)
        context = self_attend(queries, key_vecs, val_vecs)
        partial = jnp.einsum('bgrtd,grde->bte', context, wo_a.reshape(out_shape), preferred_element_type=jnp.float32).astype(jnp.bfloat16)
        h_one = (hidden.astype(jnp.float32) + scatter_sum(partial)).astype(jnp.bfloat16)
        h_two = (h_one.astype(jnp.float32) + gated_mlp(h_one, ln2_a, wg_a, wu_a, wd_a)).astype(jnp.bfloat16)
        gathered = gather_rows(rms_scale(h_two, ln1_b).astype(jnp.bfloat16))
        queries = jnp.einsum('btd,dgre->bgrte', gathered, wq_b.reshape(query_shape), preferred_element_type=jnp.float32)
        queries = rms_scale(queries, q_norm).astype(jnp.bfloat16)
        vis_full = gather_rows(vision)
        key_vecs = jnp.einsum('bsd,dge->bsge', vis_full, wk_b.reshape(head_shape), preferred_element_type=jnp.float32)
        key_vecs = rms_scale(key_vecs, k_norm).astype(jnp.bfloat16)
        val_vecs = jnp.einsum('bsd,dge->bsge', vis_full, wv_b.reshape(head_shape), preferred_element_type=jnp.float32).astype(jnp.bfloat16)
        context = cross_attend(queries, key_vecs, val_vecs, gather_rows(tile_mask) > 0)
        partial = jnp.einsum('bgrtd,grde->bte', context, wo_b.reshape(out_shape), preferred_element_type=jnp.float32).astype(jnp.bfloat16)
        row_keep = jnp.any(tile_mask > 0, axis=-1, keepdims=True).astype(jnp.float32)
        gate_vals = jnp.tanh(xgates.astype(jnp.float32))
        h_three = (h_two.astype(jnp.float32) + gate_vals[0] * row_keep * scatter_sum(partial)).astype(jnp.bfloat16)
        mlp_out = gated_mlp(h_three, ln2_b, wg_b, wu_b, wd_b)
        return (h_three.astype(jnp.float32) + gate_vals[1] * row_keep * mlp_out).astype(jnp.bfloat16)

    return jax.shard_map(body, mesh=mesh, in_specs=in_specs, out_specs=act_spec, check_vma=False)
```

profile of v0, /device:TPU:0, one launch (start us, length us, event | category | flops | bytes accessed | tf_op | source)
XLA Modules:
  0.0 355.0 jit_solution(8886428779664351550)
XLA Ops:
  8.5 1.9 fusion.67
  13.0 6.6 %all-reduce = s32[128]{0:T(128)S(1)} all-reduce(s32[128]{0:T(128)S(1)} %bitcast_dynamic-update-slice_fusion), channel_id=1, replica_groups=mesh['dp'=4,'tp'=4] {'tp'}, use_global_device_ids=true, to_apply=%add | all-reduce | flops 128 | bytes 1024
  20.5 9.0 %all-gather.6.cloned.1.call-done = bf16[1,128,5120]{2,1,0:T(8,128)(2,1)} async-done(((bf16[1,32,5120]{2,1,0:T(8,128)(2,1)}), bf16[1,128,5120]{2,1,0:T(8,128)(2,1)}) %all-gather.6.cloned.1.call-update) | async-done | bytes 1310736 | tf_op jit(solution)/shard_map/all_gather | solution.py:67
  29.5 10.4 %fusion.32 = f32[128,1280]{0,1:S(1)} fusion(bf16[5120,1280]{1,0:T(8,128)(2,1)} %param.31, bf16[1,128,5120]{2,1,0:T(8,128)(2,1)} %all-gather.6.cloned.1.call-done), kind=kOutput, calls=%fused_computation.41 | convolution fusion | flops 1677721600 | bytes 15073280
  42.5 2.7 fusion.56
  45.2 7.1 %fusion.7 = bf16[1,128,5120]{2,1,0:T(8,128)(2,1)} fusion(bf16[2,5,128,5120]{3,2,1,0:T(8,128)(2,1)} %bitcast.196, bf16[128,2,128,1]{2,0,3,1:T(8,128)(2,1)S(1)} %fusion.56, f32[2,5,128,128]{2,3,1,0:T(8,128)} %get-tuple-element.20, f32[2,5,128]{2,1,0:T(8,128)S(1)} %get-tuple-element.19), kind=kOutput, calls=%fused_computation.11 | convolution fusion | flops 1720811520 | bytes 15143936 | tf_op jit(solution)/shard_map/bgrtd,grde->bte/dot_general | solution.py:109
  52.4 22.6 %reduce-scatter.5.cloned.1.call-done = bf16[1,32,5120]{2,1,0:T(8,128)(2,1)} async-done(((bf16[1,128,5120]{2,1,0:T(8,128)(2,1)}), bf16[1,32,5120]{2,1,0:T(8,128)(2,1)}) %reduce-scatter.5.cloned.1.call-update) | async-done | bytes 327696 | tf_op jit(solution)/shard_map/reduce_scatter | solution.py:71
  77.3 16.0 %all-gather.8.cloned.1.call-done = bf16[1,128,5120]{2,1,0:T(8,128)(2,1)} async-done(((bf16[1,32,5120]{2,1,0:T(8,128)(2,1)}), bf16[1,128,5120]{2,1,0:T(8,128)(2,1)}) %all-gather.8.cloned.1.call-update) | async-done | bytes 1310736 | tf_op jit(solution)/shard_map/all_gather | solution.py:67
  93.4 17.6 %fusion.27 = f32[128,3456]{1,0:T(8,128)} fusion(bf16[5120,3456]{1,0:T(8,128)(2,1)} %param.36, bf16[1,128,5120]{2,1,0:T(8,128)(2,1)} %all-gather.8.cloned.1.call-done), kind=kOutput, calls=%fused_computation.36 | convolution fusion | flops 4529848320 | bytes 38469632 | tf_op jit(solution)/shard_map/btd,df->btf/dot_general | solution.py:76
  111.0 27.2 %fusion.4 = bf16[1,128,5120]{2,1,0:T(8,128)(2,1)} fusion(bf16[3456,5120]{1,0:T(8,128)(2,1)} %param.38, bf16[5120,3456]{1,0:T(8,128)(2,1)} %param.37, f32[128,3456]{1,0:T(8,128)} %fusion.27, bf16[1,128,5120]{2,1,0:T(8,128)(2,1)} %all-gather.8.cloned.1.call-done), kind=kOutput, calls=%fused_computation.8 | convolution fusion | flops 9063006208 | bytes 75169792 | tf_op jit(solution)/shard_map/btf,fd->btd/dot_general | solution.py:79
  138.9 22.1 %reduce-scatter.7.cloned.1.call-done = bf16[1,32,5120]{2,1,0:T(8,128)(2,1)} async-done(((bf16[1,128,5120]{2,1,0:T(8,128)(2,1)}), bf16[1,32,5120]{2,1,0:T(8,128)(2,1)}) %reduce-scatter.7.cloned.1.call-update) | async-done | bytes 327696 | tf_op jit(solution)/shard_map/reduce_scatter | solution.py:71
  164.2 5.4 %all_gather.24 = s32[1,128,4]{2,0,1:T(1,128)S(1)} all-gather(s32[1,32,4]{2,0,1:T(1,128)S(1)} %copy.77), channel_id=1, replica_groups=mesh['dp'=4,'tp'=4] {'tp'}, dimensions={1}, use_global_device_ids=true | all-gather | bytes 2560 | tf_op jit(solution)/shard_map/all_gather | solution.py:67
  170.2 30.7 %all-gather.12.cloned.1.call-done = bf16[1,512,5120]{2,1,0:T(8,128)(2,1)} async-done(((bf16[1,128,5120]{2,1,0:T(8,128)(2,1)}), bf16[1,512,5120]{2,1,0:T(8,128)(2,1)}) %all-gather.12.cloned.1.call-update) | async-done | bytes 5242896 | tf_op jit(solution)/shard_map/all_gather | solution.py:67
  200.9 5.0 %multiply_reduce_fusion.1 = (f32[512,2]{0,1:T(2,128)S(1)}, f32[512,256]{0,1}) fusion(bf16[5120,256]{1,0:T(8,128)(2,1)S(1)} %copy-done, bf16[1,512,5120]{2,1,0:T(8,128)(2,1)} %all-gather.12.cloned.1.call-done), kind=kOutput, calls=%fused_computation.88 | convolution fusion | flops 1342438400 | bytes 8392704
  207.5 10.9 %all-gather.10.cloned.1.call-done = bf16[1,128,5120]{2,1,0:T(8,128)(2,1)} async-done(((bf16[1,32,5120]{2,1,0:T(8,128)(2,1)}), bf16[1,128,5120]{2,1,0:T(8,128)(2,1)}) %all-gather.10.cloned.1.call-update) | async-done | bytes 1310736 | tf_op jit(solution)/shard_map/all_gather | solution.py:67
  218.4 8.5 %fusion.24 = f32[128,1280]{0,1:S(1)} fusion(bf16[5120,1280]{1,0:T(8,128)(2,1)} %param.40, bf16[1,128,5120]{2,1,0:T(8,128)(2,1)} %all-gather.10.cloned.1.call-done), kind=kOutput, calls=%fused_computation.33 | convolution fusion | flops 1677721600 | bytes 15073280
  227.0 2.8 fusion.131
  229.8 7.8 %fusion.6 = bf16[1,128,5120]{2,1,0:T(8,128)(2,1)} fusion(bf16[2,5,128,5120]{3,2,1,0:T(8,128)(2,1)} %bitcast.203, bf16[512,2,128,1]{2,0,3,1:T(8,128)(2,1)S(1)} %fusion.46, f32[2,5,128,512]{3,2,1,0:T(8,128)} %get-tuple-element.24, f32[2,5,128]{2,1,0:T(8,128)S(1)} %get-tuple-element.23), kind=kOutput, calls=%fused_computation.10 | convolution fusion | flops 1847623680 | bytes 17306624 | tf_op jit(solution)/shard_map/bgrtd,grde->bte/dot_general | solution.py:120
  239.7 20.7 %reduce-scatter.9.cloned.1.call-done = bf16[1,32,5120]{2,1,0:T(8,128)(2,1)} async-done(((bf16[1,128,5120]{2,1,0:T(8,128)(2,1)}), bf16[1,32,5120]{2,1,0:T(8,128)(2,1)}) %reduce-scatter.9.cloned.1.call-update) | async-done | bytes 327696 | tf_op jit(solution)/shard_map/reduce_scatter | solution.py:71
  262.9 15.9 %all-gather.14.cloned.1.call-done = bf16[1,128,5120]{2,1,0:T(8,128)(2,1)} async-done(((bf16[1,32,5120]{2,1,0:T(8,128)(2,1)}), bf16[1,128,5120]{2,1,0:T(8,128)(2,1)}) %all-gather.14.cloned.1.call-update) | async-done | bytes 1310736 | tf_op jit(solution)/shard_map/all_gather | solution.py:67
  278.8 17.6 %fusion.22 = f32[128,3456]{1,0:T(8,128)} fusion(bf16[5120,3456]{1,0:T(8,128)(2,1)} %param.47, bf16[1,128,5120]{2,1,0:T(8,128)(2,1)} %all-gather.14.cloned.1.call-done), kind=kOutput, calls=%fused_computation.31 | convolution fusion | flops 4529848320 | bytes 38469632 | tf_op jit(solution)/shard_map/btd,df->btf/dot_general | solution.py:76
  296.5 27.3 %fusion.5 = bf16[1,128,5120]{2,1,0:T(8,128)(2,1)} fusion(bf16[3456,5120]{1,0:T(8,128)(2,1)} %param.49, bf16[5120,3456]{1,0:T(8,128)(2,1)} %param.48, f32[128,3456]{1,0:T(8,128)} %fusion.22, bf16[1,128,5120]{2,1,0:T(8,128)(2,1)} %all-gather.14.cloned.1.call-done), kind=kOutput, calls=%fused_computation.9 | convolution fusion | flops 9063006208 | bytes 75169792 | tf_op jit(solution)/shard_map/btf,fd->btd/dot_general | solution.py:79
  323.8 22.7 %reduce-scatter.11.cloned.1.call-done = bf16[1,32,5120]{2,1,0:T(8,128)(2,1)} async-done(((bf16[1,128,5120]{2,1,0:T(8,128)(2,1)}), bf16[1,32,5120]{2,1,0:T(8,128)(2,1)}) %reduce-scatter.11.cloned.1.call-update) | async-done | bytes 327696 | tf_op jit(solution)/shard_map/reduce_scatter | solution.py:71
  346.6 1.9 fusion.80
  (91 shorter events, 20.3 us)
Async XLA Ops:
  6.5 194.4 %copy-start = (bf16[5120,256]{1,0:T(8,128)(2,1)S(1)}, bf16[5120,256]{1,0:T(8,128)(2,1)}, u32[]{:S(2)}) copy-start(bf16[5120,256]{1,0:T(8,128)(2,1)} %param.42) | copy-start | bytes 7864324
  6.5 23.0 %all-gather.6.cloned.1.call-start = ((), (), s32[]{:S(2)}) async-start(), calls=%async_computation.4 | async-start | bytes 1638400 | tf_op jit(solution)/shard_map/all_gather | solution.py:67
  10.4 64.6 %reduce-scatter.5.cloned.1.call-start = ((), (), s32[]{:S(2)}) async-start(), calls=%async_computation.5 | async-start | bytes 1638400 | tf_op jit(solution)/shard_map/reduce_scatter | solution.py:71
  29.5 10.5 %copy-start.2 = (bf16[1,128,5120]{2,1,0:T(8,128)(2,1)S(1)}, bf16[1,128,5120]{2,1,0:T(8,128)(2,1)}, u32[]{:S(2)}) copy-start(bf16[1,128,5120]{2,1,0:T(8,128)(2,1)} %all-gather.6.cloned.1.call-done) | copy-start | bytes 3932164
  29.5 10.5 %copy-start.5 = (bf16[5120,256]{1,0:T(8,128)(2,1)S(1)}, bf16[5120,256]{1,0:T(8,128)(2,1)}, u32[]{:S(2)}) copy-start(bf16[5120,256]{1,0:T(8,128)(2,1)} %param.32) | copy-start | bytes 7864324
  45.1 7.2 %copy-start.6 = (bf16[5120]{0:T(1024)(128)(2,1)S(1)}, bf16[5120]{0:T(1024)(128)(2,1)}, u32[]{:S(2)}) copy-start(bf16[5120]{0:T(1024)(128)(2,1)} %param.35) | copy-start | bytes 30724
  45.2 29.9 %copy-start.3 = (bf16[1,32,5120]{2,1,0:T(8,128)(2,1)S(1)}, bf16[1,32,5120]{2,1,0:T(8,128)(2,1)}, u32[]{:S(2)}) copy-start(bf16[1,32,5120]{2,1,0:T(8,128)(2,1)} %param.26) | copy-start | bytes 983044
  52.3 41.1 %all-gather.8.cloned.1.call-start = ((), (), s32[]{:S(2)}) async-start(), calls=%async_computation.6 | async-start | bytes 1638400 | tf_op jit(solution)/shard_map/all_gather | solution.py:67
  77.1 83.9 %reduce-scatter.7.cloned.1.call-start = ((), (), s32[]{:S(2)}) async-start(), calls=%async_computation.7 | async-start | bytes 1638400 | tf_op jit(solution)/shard_map/reduce_scatter | solution.py:71
  138.2 25.9 %copy-start.9 = (s32[1,32,4]{1,2,0:T(4,128)S(1)}, s32[1,32,4]{1,2,0:T(4,128)}, u32[]{:S(2)}) copy-start(s32[1,32,4]{1,2,0:T(4,128)} %param.29) | copy-start | bytes 1540
  138.2 31.9 %copy-start.12 = (bf16[128]{0:T(256)(128)(2,1)S(1)}, bf16[128]{0:T(256)(128)(2,1)}, u32[]{:S(2)}) copy-start(bf16[128]{0:T(256)(128)(2,1)} %param.44) | copy-start | bytes 772
  138.2 31.9 %copy-start.13 = (bf16[128]{0:T(256)(128)(2,1)S(1)}, bf16[128]{0:T(256)(128)(2,1)}, u32[]{:S(2)}) copy-start(bf16[128]{0:T(256)(128)(2,1)} %param.41) | copy-start | bytes 772
  138.3 62.6 %all-gather.12.cloned.1.call-start = ((), (), s32[]{:S(2)}) async-start(), calls=%async_computation.9 | async-start | bytes 6553600 | tf_op jit(solution)/shard_map/all_gather | solution.py:67
  138.9 79.5 %all-gather.10.cloned.1.call-start = ((), (), s32[]{:S(2)}) async-start(), calls=%async_computation.8 | async-start | bytes 1638400 | tf_op jit(solution)/shard_map/all_gather | solution.py:67
  164.0 96.3 %reduce-scatter.9.cloned.1.call-start = ((), (), s32[]{:S(2)}) async-start(), calls=%async_computation.10 | async-start | bytes 1638400 | tf_op jit(solution)/shard_map/reduce_scatter | solution.py:71
  200.9 5.0 %copy-start.10 = (bf16[1,512,5120]{2,1,0:T(8,128)(2,1)S(1)}, bf16[1,512,5120]{2,1,0:T(8,128)(2,1)}, u32[]{:S(2)}) copy-start(bf16[1,512,5120]{2,1,0:T(8,128)(2,1)} %all-gather.12.cloned.1.call-done) | copy-start | bytes 15728644
  200.9 5.0 %copy-start.11 = (bf16[5120,256]{1,0:T(8,128)(2,1)S(1)}, bf16[5120,256]{1,0:T(8,128)(2,1)}, u32[]{:S(2)}) copy-start(bf16[5120,256]{1,0:T(8,128)(2,1)} %param.43) | copy-start | bytes 7864324
  207.4 19.6 %copy-start.15 = (f32[512,256]{0,1:S(1)}, f32[512,256]{0,1}, u32[]{:S(2)}) copy-start(f32[512,256]{0,1} %get-tuple-element.22) | copy-start | bytes 1572868
  229.8 7.9 %copy-start.14 = (f32[2]{0:T(128)S(1)}, f32[2]{0:T(128)}, u32[]{:S(2)}) copy-start(f32[2]{0:T(128)} %param.50) | copy-start | bytes 28
  229.8 7.9 %copy-start.8 = (bf16[5120]{0:T(1024)(128)(2,1)S(1)}, bf16[5120]{0:T(1024)(128)(2,1)}, u32[]{:S(2)}) copy-start(bf16[5120]{0:T(1024)(128)(2,1)} %param.46) | copy-start | bytes 30724
  229.8 30.6 %copy-start.4 = (bf16[1,32,5120]{2,1,0:T(8,128)(2,1)S(1)}, bf16[1,32,5120]{2,1,0:T(8,128)(2,1)}, u32[]{:S(2)}) copy-start(bf16[1,32,5120]{2,1,0:T(8,128)(2,1)} %reduce-scatter.7.cloned.1.call-done) | copy-start | bytes 983044
  237.7 41.2 %all-gather.14.cloned.1.call-start = ((), (), s32[]{:S(2)}) async-start(), calls=%async_computation.11 | async-start | bytes 1638400 | tf_op jit(solution)/shard_map/all_gather | solution.py:67
  262.6 84.0 %reduce-scatter.11.cloned.1.call-start = ((), (), s32[]{:S(2)}) async-start(), calls=%async_computation.12 | async-start | bytes 1638400 | tf_op jit(solution)/shard_map/reduce_scatter | solution.py:71
  296.5 52.0 %copy-start.1 = (bf16[5120,256]{1,0:T(8,128)(2,1)S(1)}, bf16[5120,256]{1,0:T(8,128)(2,1)}, u32[]{:S(2)}) copy-start(bf16[5120,256]{1,0:T(8,128)(2,1)} %param.42) | copy-start | bytes 7864324
  (1 other events, 0.7 us)
Sparse Core Ops, SparseCore 0:
  10.5 18.8 all-gather.5
  52.4 22.5 reduce-scatter.4
  77.2 16.0 all-gather.7
  138.4 22.5 reduce-scatter.6
  162.4 38.4 all-gather.11
  202.3 16.0 all-gather.9
  237.8 22.5 reduce-scatter.8
  262.7 16.0 all-gather.13
  324.0 22.5 reduce-scatter.10
where the time goes:
time: 355 us
  waiting for transfers between devices  171 us (48%)
  matrix products  138 us (39%)
  other arithmetic  15.5 us (4%)
  between operations  14.1 us (4%)
  blocking collectives  12.1 us (3%)
    reduce_scatter x4, waiting for transfers between devices, scatter_sum(): lax.psum_scatter(partial, 'tp', scatter_dimension=1, tiled=True)  88.1 us
    all_gather x5, waiting for transfers between devices, gather_rows(): return lax.all_gather(values, 'tp', axis=1, tiled=True)  82.6 us
    dot_general x2, matrix products, gated_mlp(): jnp.einsum('btf,fd->btd', activated, w_down, preferred_element_type=jnp.f...  54.6 us
    dot_general x2, matrix products, gated_mlp(): jnp.einsum('btd,df->btf', gathered, w_gate, preferred_element_type=jnp.fl...  35.3 us
    unnamed x4, matrix products  25.1 us
    dot_general x1, matrix products, body(): jnp.einsum('bgrtd,grde->bte', context, wo_b.reshape(out_shape), preferred...  7.84 us
  transfers between devices with their start and end apart: 9, of which 9 were waited for; matrix products, arithmetic and copies ran while one was open for 4% of the time, Pallas kernels for 0%

commit v1 on v0

v1 whole, which is shorter than its diff:
```python
import functools
import math

import jax
import jax.numpy as jnp
from jax import lax
from jax.experimental import pallas as pl
from jax.experimental.pallas import tpu as pltpu
from jax.sharding import PartitionSpec as P

ROPE_THETA = 500000.0
ROPE_FACTOR = 8.0
LOW_FACTOR = 1.0
HIGH_FACTOR = 4.0
ORIG_CONTEXT = 8192.0
NORM_EPS = 1e-5
MASK_VALUE = -1e30
MESH = pl.DeviceIdType.MESH
F32 = jnp.float32
BF16 = jnp.bfloat16

D = 5120
TOK = 128
HD = 128
HEADS = 10
GROUPS = 2
REP = 5
FF = 3456
TILES = 4
CH = 10
CW = D // CH
HW = CW // 2
UNIT = 128
RING = 1440
AGC = 4
VCH = 8
VROWS = TOK // VCH

SEG = {
    "qkv_a": (0, 560, 1),
    "o_a": (560, 40, 10),
    "gu_a": (960, 80, 27),
    "d_a": (3120, 120, 10),
    "kv_b": (4320, 160, 1),
    "q_b": (4480, 40, 10),
    "o_b": (4880, 40, 10),
    "gu_b": (5280, 80, 27),
    "d_b": (7440, 120, 10),
}
SEMS = {"qkv_a": 0, "o_a": 2, "gu_a": 12, "d_a": 21, "kv_b": 31, "q_b": 32, "o_b": 34, "gu_b": 44, "d_b": 53}
NSEM = 63


def rope_table(head_dim):
    low_wave = ORIG_CONTEXT / LOW_FACTOR
    high_wave = ORIG_CONTEXT / HIGH_FACTOR
    freq_list = []
    for freq_idx in range(head_dim // 2):
        base_freq = 1.0 / (ROPE_THETA ** (2.0 * freq_idx / head_dim))
        wave_len = 2.0 * math.pi / base_freq
        if wave_len > low_wave:
            freq_list.append(base_freq / ROPE_FACTOR)
        elif wave_len < high_wave:
            freq_list.append(base_freq)
        else:
            smooth = (ORIG_CONTEXT / wave_len - LOW_FACTOR) / (HIGH_FACTOR - LOW_FACTOR)
            freq_list.append((1.0 - smooth) * base_freq / ROPE_FACTOR + smooth * base_freq)
    return jnp.array(freq_list, dtype=jnp.float32)


def head_norm(values, gain):
    mean_sq = jnp.mean(values * values, axis=-1, keepdims=True)
    return values * lax.rsqrt(mean_sq + NORM_EPS) * gain


def softmax_rows(scores):
    top = jnp.max(scores, axis=-1, keepdims=True)
    weights = jnp.exp(scores - top)
    return (weights / jnp.sum(weights, axis=-1, keepdims=True)).astype(BF16)


def dot_nt(left, right):
    return lax.dot_general(left, right, (((1,), (1,)), ((), ())), preferred_element_type=F32)


def kernel(pos, tmask, gains, small, hid, vis, wq_a, wk_a, wv_a, wo_a, wg_a, wu_a, wd_a, wq_b, wk_b, wv_b, wo_b, wg_b, wu_b, wd_b, out,
           ring, hbuf, xn, vbuf, meta, cos_s, sin_s, fac, qs, ks, vs, kb, vb, ctx, act, pall, psib, csum, crcv, ostage, fin,
           wsem, lsem, ag_s, ag_r, mt_s, mt_r, vx_s, vx_r, vr_s, vr_r, vo_s, vo_r, ps_s, ps_r, cs_s, cs_r, hh_s, hh_r):
    me = lax.axis_index("tp")
    xi = lax.div(me, 2)
    co = lax.rem(me, 2)
    sib = xi * 2 + 1 - co
    cross = (1 - xi) * 2 + co
    diag = (1 - xi) * 2 + 1 - co

    def remote(src, dst, ssem, rsem, dev):
        return pltpu.make_async_remote_copy(src_ref=src, dst_ref=dst, send_sem=ssem, recv_sem=rsem, device_id={"tp": dev}, device_id_type=MESH)

    def spot(name, j):
        first, units, _ = SEG[name]
        return lax.rem(first + j * units, RING) * UNIT

    def put(weight, rows, col, at, sem):
        pltpu.make_async_copy(weight.at[:, pl.ds(pl.multiple_of(col * 128, 128), 128)], ring.at[pl.ds(pl.multiple_of(at, 128), rows)], sem).start()

    def start_group(name, j):
        at = spot(name, j)
        base = SEMS[name]
        if name[:2] == "o_":
            for p in range(4):
                put(wo_a if name == "o_a" else wo_b, 1280, j * 4 + p, at + p * 1280, wsem.at[base + j])
        elif name[:2] == "gu":
            sem = wsem.at[base + lax.div(j, 3)]
            put(wg_a if name == "gu_a" else wg_b, D, j, at, sem)
            put(wu_a if name == "gu_a" else wu_b, D, j, at + D, sem)
        elif name[:2] == "d_":
            for p in range(4):
                put(wd_a if name == "d_a" else wd_b, FF, j * 4 + p, at + p * 30 * UNIT, wsem.at[base + j])
        elif name == "q_b":
            put(wq_b, D, j, at, wsem.at[base + lax.div(j, 8)])
        elif name == "kv_b":
            for p, w in enumerate((wk_b, wk_b, wv_b, wv_b)):
                put(w, D, p % 2, at + p * D, wsem.at[base])
        else:
            for p in range(14):
                w = wq_a if p < 10 else (wk_a if p < 12 else wv_a)
                put(w, D, p if p < 10 else p % 2, at + p * D, wsem.at[base + p // 8])

    def ready(name, freed):
        first, units, count = SEG[name]
        if isinstance(freed, int):
            return min(max((freed + RING - first) // units, 0), count)
        return jnp.minimum(jnp.maximum(lax.div(freed + RING - first + 100 * units, units) - 100, 0), count)

    def refill(before, after, low, high):
        for name, (first, units, count) in SEG.items():
            if first + units > high + RING or first + units * count <= low + RING:
                continue
            lo, hi = ready(name, before), ready(name, after)
            if isinstance(lo, int) and isinstance(hi, int) and lo >= hi:
                continue
            lax.fori_loop(lo, hi, lambda j, _, name=name: (start_group(name, j), 0)[1], 0)

    def landed(at, rows, sem):
        span = ring.at[pl.ds(pl.multiple_of(at, 128), rows)]
        pltpu.make_async_copy(span, span, sem).wait()

    def panels(at, rows, pitch, count):
        return jnp.concatenate([ring[pl.ds(pl.multiple_of(at + p * pitch, 128), rows), :] for p in range(count)], axis=1)

    def mm(left, right):
        return jnp.dot(left, right, preferred_element_type=F32)

    own_rows = pl.ds(pl.multiple_of(me * 32, 32), 32)
    load_h = pltpu.make_async_copy(hid.at[0], hbuf.at[own_rows], lsem.at[0])
    load_h.start()
    load_v = pltpu.make_async_copy(vis.at[0], vbuf.at[me], lsem.at[1])
    barrier = pltpu.get_barrier_semaphore()
    for dev in (sib, cross, diag):
        pl.semaphore_signal(barrier, inc=1, device_id={"tp": dev}, device_id_type=MESH)
    for name in SEG:
        for j in range(ready(name, 0) if name == "qkv_a" else 0):
            start_group(name, j)
    row_i = lax.broadcasted_iota(jnp.int32, (32, 128), 0)
    lane_i = lax.broadcasted_iota(jnp.int32, (32, 128), 1)
    pos_row = jnp.concatenate([jnp.broadcast_to(pos[...].astype(F32), (32, 32)), jnp.zeros((32, 96), F32)], axis=1)
    pos_col = jnp.sum(jnp.where(row_i == lane_i, pos_row, 0.0), axis=1, keepdims=True)
    own_meta = jnp.where(lane_i == 0, pos_col, 0.0)
    tm = tmask[0].astype(F32)
    for j in range(TILES):
        own_meta = jnp.where(lane_i == j + 1, tm[:, j:j + 1], own_meta)
    meta[own_rows, :] = own_meta
    load_h.wait()
    pl.semaphore_wait(barrier, 3)

    def ag(kind, k):
        cols = pl.ds(k * (D // AGC), D // AGC)
        rows = pl.ds(pl.multiple_of((cross if kind == 2 else me) * 32, 32), 32)
        ref = hbuf.at[rows, cols]
        return remote(ref, ref, ag_s.at[kind, k], ag_r.at[kind, k], cross if kind == 1 else sib)

    for k in range(AGC):
        ag(1, k).start()
    for k in range(AGC):
        ag(0, k).start()
    metas = [remote(meta.at[own_rows], meta.at[own_rows], mt_s.at[i], mt_r.at[i], dev) for i, dev in enumerate((sib, cross, diag))]
    for m in metas:
        m.start()
    load_v.start()
    refill(-RING, 0, 560 - RING, 0)

    def norm_rows(first, count, gain):
        def block(b, _):
            rows = pl.ds(pl.multiple_of(first + b * 16, 16), 16)
            v = hbuf[rows, :].astype(F32)
            scale = lax.rsqrt(jnp.mean(v * v, axis=-1, keepdims=True) + NORM_EPS)
            xn[rows, :] = (v * scale * gains[gain:gain + 1, :]).astype(BF16)
            return 0
        lax.fori_loop(0, count // 16, block, 0)

    norm_rows(me * 32, 32, 0)
    for k in range(AGC):
        ag(0, k).wait_recv()
    norm_rows(sib * 32, 32, 0)
    for m in metas:
        m.wait_recv()
    angles = meta[:, 0:1] * small[2:3, :]
    cos_s[...] = jnp.cos(angles)
    lanes = lax.broadcasted_iota(jnp.int32, (TOK, HD), 1)
    sin_s[...] = jnp.where(lanes < HD // 2, -jnp.sin(angles), jnp.sin(angles))
    keep = jnp.max(jnp.where((lanes >= 1) & (lanes <= TILES), meta[...], 0.0), axis=1, keepdims=True)
    fac[0] = jnp.broadcast_to(jnp.where(keep > 0.0, 1.0, 0.0) * small[3:4, 0:1], (TOK, HW))
    fac[1] = jnp.broadcast_to(jnp.where(keep > 0.0, 1.0, 0.0) * small[4:5, 0:1], (TOK, HW))
    for k in range(AGC):
        ag(1, k).wait_recv()
        ag(2, k).start()
    norm_rows(cross * 32, 32, 0)

    load_v.wait()

    def vown():
        return remote(vbuf.at[me], vbuf.at[me], vo_s, vo_r, sib)

    def vcross(k):
        ref = vbuf.at[me, pl.ds(k * VROWS, VROWS), :]
        return remote(ref, ref, vx_s.at[k], vx_r.at[k], cross)

    def vrelay(k):
        ref = vbuf.at[cross, pl.ds(k * VROWS, VROWS), :]
        return remote(ref, ref, vr_s.at[k], vr_r.at[k], sib)

    for k in range(0, 2):
        vcross(k).start()
    for k in range(AGC):
        ag(2, k).wait_recv()
    norm_rows(diag * 32, 32, 0)
    vown().start()

    def rope(v):
        return (v * cos_s[...] + pltpu.roll(v, HD // 2, 1) * sin_s[...]).astype(BF16)

    at = spot("qkv_a", 0)
    landed(at, 8 * D, wsem.at[0])
    r = mm(xn[...], panels(at, D, D, 8))
    for i in range(8):
        qs[i] = rope(r[:, i * HD:(i + 1) * HD])
    landed(at + 8 * D, 6 * D, wsem.at[1])
    r = mm(xn[...], panels(at + 8 * D, D, D, 6))
    for i in range(2):
        qs[8 + i] = rope(r[:, i * HD:(i + 1) * HD])
        ks[i] = rope(r[:, (2 + i) * HD:(3 + i) * HD])
        vs[i] = r[:, (4 + i) * HD:(5 + i) * HD].astype(BF16)
    refill(0, 560, 0, 560)

    causal = lax.broadcasted_iota(jnp.int32, (TOK, TOK), 0) >= lax.broadcasted_iota(jnp.int32, (TOK, TOK), 1)
    for i in range(HEADS):
        g = i // REP
        scores = dot_nt(qs[i], ks[g]) * (HD ** -0.5)
        weights = softmax_rows(jnp.where(causal, scores, MASK_VALUE))
        ctx[:, i * HD:(i + 1) * HD] = mm(weights, vs[g]).astype(BF16)

    def to_sib(n):
        return remote(pall.at[n, 1 - co], psib.at[n], ps_s.at[n], ps_r.at[n], sib)

    def to_cross(n, par, half):
        if half:
            rows = pl.ds(pl.multiple_of((1 - xi) * 64, 64), 64)
            return remote(csum.at[n, rows], crcv.at[par, n, rows], cs_s.at[n], cs_r.at[par, n], cross)
        return remote(csum.at[n], crcv.at[par, n], cs_s.at[n], cs_r.at[par, n], cross)

    def half_cols(n):
        return pl.ds(pl.multiple_of(n * CW + co * HW, HW), HW)

    def h_out(n):
        ref = hbuf.at[:, half_cols(n)]
        return remote(ref, ref, hh_s.at[n], hh_r.at[n], sib)

    def each(fn):
        lax.fori_loop(0, CH, lambda n, _: (fn(n), 0)[1], 0)

    def reduce_out(name, left, rows, pitch, par, half):
        first, units, _ = SEG[name]

        def pair_sum(n):
            to_sib(n).wait_recv()
            csum[n] = (pall[n, co].astype(F32) + psib[n].astype(F32)).astype(BF16)
            to_cross(n, par, half).start()

        def chunk(n):
            start = spot(name, n)
            landed(start, 4 * rows, wsem.at[SEMS[name] + n])
            part = mm(left[...], panels(start, rows, pitch, 4))
            pall[n, 0] = part[:, :HW].astype(BF16)
            pall[n, 1] = part[:, HW:].astype(BF16)
            to_sib(n).start()
            refill(first + n * units, first + (n + 1) * units, first, first + CH * units)

            @pl.when(n >= 1)
            def _():
                pair_sum(n - 1)

        each(chunk)
        pair_sum(CH - 1)

    def finish(par, factor):
        def chunk(n):
            to_cross(n, par, False).wait_recv()
            total = csum[n].astype(F32) + crcv[par, n].astype(F32)
            if factor is not None:
                total = fac[factor] * total
            cols = half_cols(n)
            hbuf[:, cols] = (hbuf[:, cols].astype(F32) + total).astype(BF16)
            h_out(n).start()

        each(chunk)

        def settle(n):
            h_out(n).wait_recv()
            h_out(n).wait_send()
            to_sib(n).wait_send()
            to_cross(n, par, False).wait_send()

        each(settle)

    def gate_up(name):
        first = SEG[name][0]

        def step(i, _):
            start = spot(name, i * 3)
            landed(start, 6 * D, wsem.at[SEMS[name] + i])
            part = mm(xn[...], panels(start, D, D, 6))
            for p in range(3):
                gate = part[:, p * 256:p * 256 + 128]
                up = part[:, p * 256 + 128:p * 256 + 256]
                act[:, pl.ds(pl.multiple_of((i * 3 + p) * 128, 128), 128)] = (jax.nn.silu(gate) * up).astype(BF16)
            refill(first + i * 240, first + (i + 1) * 240, first, first + 2160)
            return 0

        lax.fori_loop(0, 9, step, 0)

    for k in range(AGC):
        for kind in range(3):
            ag(kind, k).wait_send()
    reduce_out("o_a", ctx, 1280, 1280, 0, False)
    finish(0, None)
    for k in range(2, 5):
        vcross(k).start()
    for k in range(0, 2):
        vcross(k).wait_recv()
        vrelay(k).start()
    norm_rows(0, TOK, 1)
    gate_up("gu_a")
    reduce_out("d_a", act, FF, 30 * UNIT, 1, False)
    for k in range(5, VCH):
        vcross(k).start()

    kv_at = spot("kv_b", 0)

    def kv_block(b):
        part = mm(vbuf[b], panels(kv_at, D, D, 4))
        rows = pl.ds(pl.multiple_of(b * TOK, TOK), TOK)
        for g in range(GROUPS):
            kb[g, rows, :] = head_norm(part[:, g * HD:(g + 1) * HD], small[1:2, :]).astype(BF16)
            vb[g, rows, :] = part[:, (2 + g) * HD:(3 + g) * HD].astype(BF16)

    landed(kv_at, 4 * D, wsem.at[SEMS["kv_b"]])
    vown().wait_recv()
    lax.fori_loop(0, 2, lambda i, _: (kv_block(me + i * (sib - me)), 0)[1], 0)
    for k in range(2, 5):
        vcross(k).wait_recv()
        vrelay(k).start()
    finish(1, None)
    norm_rows(0, TOK, 2)

    at = spot("q_b", 0)
    landed(at, 8 * D, wsem.at[SEMS["q_b"]])
    r = mm(xn[...], panels(at, D, D, 8))
    for i in range(8):
        qs[i] = head_norm(r[:, i * HD:(i + 1) * HD], small[0:1, :]).astype(BF16)
    landed(at + 8 * D, 2 * D, wsem.at[SEMS["q_b"] + 1])
    r = mm(xn[...], panels(at + 8 * D, D, D, 2))
    for i in range(2):
        qs[8 + i] = head_norm(r[:, i * HD:(i + 1) * HD], small[0:1, :]).astype(BF16)
    for k in range(5, VCH):
        vcross(k).wait_recv()
        vrelay(k).start()
    for k in range(VCH):
        vrelay(k).wait_recv()
    lax.fori_loop(0, 2, lambda i, _: (kv_block(cross + i * (diag - cross)), 0)[1], 0)
    refill(4320, 4880, 4320, 4880)

    def cross_group(g, _):
        for i in range(REP):
            scores = dot_nt(qs[g * REP + i], kb[g]) * (HD ** -0.5)
            scores = jnp.concatenate(
                [jnp.where(meta[:, j + 1:j + 2] > 0.0, scores[:, j * HD:(j + 1) * HD], MASK_VALUE) for j in range(TILES)], axis=1)
            ctx[:, pl.ds(pl.multiple_of((g * REP + i) * HD, HD), HD)] = mm(softmax_rows(scores), vb[g]).astype(BF16)
        return 0

    lax.fori_loop(0, GROUPS, cross_group, 0)
    reduce_out("o_b", ctx, 1280, 1280, 0, False)
    finish(0, 0)
    norm_rows(0, TOK, 3)
    gate_up("gu_b")
    reduce_out("d_b", act, FF, 30 * UNIT, 1, True)

    chip_rows = pl.ds(pl.multiple_of(xi * 64, 64), 64)

    def fin_out(n):
        return remote(ostage.at[n, pl.ds(pl.multiple_of((1 - co) * 32, 32), 32)], fin.at[:, half_cols(n)], hh_s.at[n], hh_r.at[n], sib)

    def last(n):
        to_cross(n, 1, True).wait_recv()
        cols = half_cols(n)
        total = csum[n, chip_rows].astype(F32) + crcv[1, n, chip_rows].astype(F32)
        ostage[n] = (hbuf[chip_rows, cols].astype(F32) + fac[1, chip_rows] * total).astype(BF16)
        fin_out(n).start()
        fin[:, cols] = ostage[n, pl.ds(pl.multiple_of(co * 32, 32), 32), :]

    each(last)

    def settle(n):
        fin_out(n).wait_recv()
        fin_out(n).wait_send()
        to_sib(n).wait_send()
        to_cross(n, 1, True).wait_send()

    each(settle)
    store = pltpu.make_async_copy(fin, out.at[0], lsem.at[2])
    store.start()
    for m in metas:
        m.wait_send()
    vown().wait_send()
    for k in range(VCH):
        vcross(k).wait_send()
        vrelay(k).wait_send()
    store.wait()


def solution(mesh):
    act_spec = P('dp', 'tp', None)
    col_spec = P(None, 'tp')
    row_spec = P('tp', None)
    layer_a = (P(), col_spec, col_spec, col_spec, row_spec, P(), col_spec, col_spec, row_spec)
    layer_b = (P(), col_spec, P(), col_spec, col_spec, P(), row_spec, P(), col_spec, col_spec, row_spec, P())
    in_specs = (act_spec, act_spec, P('dp', 'tp'), act_spec) + layer_a + layer_b

    def body(hidden, vision, positions, tile_mask, ln1_a, wq_a, wk_a, wv_a, wo_a, ln2_a, wg_a, wu_a, wd_a, ln1_b, wq_b, q_norm, wk_b, wv_b, k_norm, wo_b, ln2_b, wg_b, wu_b, wd_b, xgates):
        gains = jnp.stack([ln1_a, ln2_a, ln1_b, ln2_b]).astype(F32)
        gate_vals = jnp.tanh(xgates.astype(F32))
        freq = rope_table(HD)
        ones = jnp.ones((HD,), F32)
        small = jnp.stack([q_norm.astype(F32), k_norm.astype(F32), jnp.concatenate([freq, freq]), gate_vals[0] * ones, gate_vals[1] * ones])
        vmem = pl.BlockSpec(memory_space=pltpu.VMEM)
        hbm = pl.BlockSpec(memory_space=pl.ANY)
        dma = pltpu.SemaphoreType.DMA
        return pl.pallas_call(
            kernel,
            out_shape=jax.ShapeDtypeStruct((1, 32, D), BF16),
            in_specs=[vmem] * 4 + [hbm] * 16,
            out_specs=hbm,
            scratch_shapes=[
                pltpu.VMEM((RING * UNIT, 128), BF16),
                pltpu.VMEM((TOK, D), BF16),
                pltpu.VMEM((TOK, D), BF16),
                pltpu.VMEM((4, TOK, D), BF16),
                pltpu.VMEM((TOK, 128), F32),
                pltpu.VMEM((TOK, HD), F32),
                pltpu.VMEM((TOK, HD), F32),
                pltpu.VMEM((2, TOK, HW), F32),
                pltpu.VMEM((HEADS, TOK, HD), BF16),
                pltpu.VMEM((GROUPS, TOK, HD), BF16),
                pltpu.VMEM((GROUPS, TOK, HD), BF16),
                pltpu.VMEM((GROUPS, 4 * TOK, HD), BF16),
                pltpu.VMEM((GROUPS, 4 * TOK, HD), BF16),
                pltpu.VMEM((TOK, HEADS * HD), BF16),
                pltpu.VMEM((TOK, FF), BF16),
                pltpu.VMEM((CH, 2, TOK, HW), BF16),
                pltpu.VMEM((CH, TOK, HW), BF16),
                pltpu.VMEM((CH, TOK, HW), BF16),
                pltpu.VMEM((2, CH, TOK, HW), BF16),
                pltpu.VMEM((CH, 64, HW), BF16),
                pltpu.VMEM((32, D), BF16),
                dma((NSEM,)), dma((3,)),
                dma((3, AGC)), dma((3, AGC)),
                dma((3,)), dma((3,)),
                dma((VCH,)), dma((VCH,)),
                dma((VCH,)), dma((VCH,)),
                dma(()), dma(()),
                dma((CH,)), dma((CH,)),
                dma((CH,)), dma((2, CH)),
                dma((CH,)), dma((CH,)),
            ],
            compiler_params=pltpu.CompilerParams(collective_id=0, has_side_effects=True, vmem_limit_bytes=67043328),
        )(positions, tile_mask, gains, small, hidden, vision, wq_a, wk_a, wv_a, wo_a, wg_a, wu_a, wd_a, wq_b, wk_b, wv_b, wo_b, wg_b, wu_b, wd_b)

    return jax.shard_map(body, mesh=mesh, in_specs=in_specs, out_specs=act_spec, check_vma=False)
```

time: 355 us -> 148 us (0.42)
  waiting for transfers between devices: 171 us -> 0 us
  matrix products: 138 us -> 0 us
  Pallas kernels: 0 us -> 136 us
  other arithmetic: 15.5 us -> 1.41 us
  between operations: 14.1 us -> 0.04 us
  blocking collectives: 12.1 us -> 0 us
  local copies, waits for them, and re-layouts: 3.19 us -> 9.74 us
    pallas_call x0 -> x1, Pallas kernels: none -> 136 us  [body(): pl.pallas_call(kernel, out_shape=jax.ShapeDtypeStruct((1, 32, D), BF16),...]
    dot_general x8 -> x0, matrix products: 109 us -> none  [the longest x2 54.6 us: gated_mlp(): jnp.einsum('btf,fd->btd', activated, w_down, preferred_element_type=jnp.f...]
    reduce_scatter x4 -> x0, waiting for transfers between devices: 88.1 us -> none  [scatter_sum(): lax.psum_scatter(partial, 'tp', scatter_dimension=1, tiled=True)]
    all_gather x5 -> x0, waiting for transfers between devices: 82.6 us -> none  [gather_rows(): return lax.all_gather(values, 'tp', axis=1, tiled=True)]
    unnamed x4 -> x0, matrix products: 25.1 us -> none
    convert_element_type x12 -> x1, other arithmetic: 8.19 us -> 0.74 us  [body(): gains = jnp.stack([ln1_a, ln2_a, ln1_b, ln2_b]).astype(F32)]
    unnamed x1 -> x0, blocking collectives: 6.64 us -> none
    all_gather x1 -> x0, blocking collectives: 5.44 us -> none  [gather_rows(): return lax.all_gather(values, 'tp', axis=1, tiled=True)]
  transfers between devices with their start and end apart: 9 -> 0, of which waited for: 9 -> 0; matrix products, arithmetic and copies ran while one was open for 4% -> 0% of each run, Pallas kernels for 0% -> 0%
where the time goes in v1:
time: 148 us; the launch traced here: 147 us
  Pallas kernels  136 us (92%)
  local copies, waits for them, and re-layouts  9.74 us (7%)
    pallas_call x1, Pallas kernels, body(): pl.pallas_call(kernel, out_shape=jax.ShapeDtypeStruct((1, 32, D), BF16),...  136 us
    unnamed x2, local copies, waits for them, and re-layouts  3.08 us

profile of v1, /device:TPU:0, one launch (start us, length us, event | category | flops | bytes accessed | tf_op | source)
XLA Modules:
  0.0 147.4 jit_solution(4321303875430616700)
XLA Ops:
  0.0 0.7 tanh.3
  0.7 0.6 fusion
  1.2 0.6 stack.50
  1.9 0.6 stack.49
  2.5 0.7 bitcast_convert_fusion
  3.2 1.3 stack.51.small
  4.5 1.4 copy.27.tmask
  5.9 0.7 stack.39
  6.6 0.7 stack.40
  7.3 0.7 stack.41
  8.0 0.7 stack.42
  8.7 0.7 maximum_convert_fusion.gains
  9.5 136.2 %shard_map.244 = bf16[1,32,5120]{2,1,0:T(8,128)(2,1)} custom-call(s32[1,32]{1,0:T(1,128)} %pos.1, s32[1,32,4]{2,1,0:T(8,128)} %copy.27.tmask, f32[4,5120]{1,0:T(4,128)} %maximum_convert_fusion.gains, f32[5,128]{1,0:T(8,128)} %stack.51.small, bf16[1,32,5120]{2,1,0:T(8,128)(2,1)} %hid.1, bf16[1,128,5120]{2,1,0:T(8,128)(2,1)} %vis.1, bf16[5120,1280]{1,0:T(8,128)(2,1)} %wq_a.1, ...), custom_call_target="tpu_custom_call" | custom-call | tf_op jit(solution)/shard_map/pallas_call | solution.py:457
  145.7 1.7 %copy.29 = bf16[1,32,5120]{2,1,0:T(8,128)(2,1)} copy(bf16[1,32,5120]{2,1,0:T(8,128)(2,1)} %shard_map.244) | data formatting | bytes 655360

commit v2 on v1

v2 whole, which is shorter than its diff:
```python
import math

import jax
import jax.numpy as jnp
import numpy as np
from jax import lax
from jax.experimental import pallas as pl
from jax.experimental.pallas import tpu as pltpu
from jax.sharding import PartitionSpec as P

ROPE_THETA = 500000.0
ROPE_FACTOR = 8.0
LOW_FACTOR = 1.0
HIGH_FACTOR = 4.0
ORIG_CONTEXT = 8192.0
NORM_EPS = 1e-5
MASK_VALUE = -1e30
MESH = pl.DeviceIdType.MESH
F32 = jnp.float32
BF16 = jnp.bfloat16

D = 5120
TOK = 128
HD = 128
HEADS = 10
GROUPS = 2
REP = 5
FF = 3456
TILES = 4
CH = 10
CW = D // CH
HW = CW // 2
OWN = 32
PAIR = 64
KT = 40
QW = 1280
SUB = 16
UNIT = 128
RING = 1440
AGC = 4
VCH = 16
VGROUP = (0, 5, 14, 16)
EARLY = 112

SEG = {
    "qkv_a": (0, 560, 1),
    "o_a": (560, 40, 10),
    "gu_a": (960, 80, 27),
    "d_a": (3120, 120, 10),
    "q_b": (4320, 40, 10),
    "kv_b": (4720, 160, 1),
    "o_b": (4880, 40, 10),
    "gu_b": (5280, 240, 10),
    "d_b": (7680, 120, 10),
}
SEMS = {"qkv_a": 0, "q_b": 0, "o_a": 2, "o_b": 2, "d_a": 12, "d_b": 12, "gu_a": 22, "gu_b": 22, "kv_b": 40}
NSEM = 41
GU_SEMS = 18


def rope_table(head_dim):
    low_wave = ORIG_CONTEXT / LOW_FACTOR
    high_wave = ORIG_CONTEXT / HIGH_FACTOR
    freq_list = []
    for freq_idx in range(head_dim // 2):
        base_freq = 1.0 / (ROPE_THETA ** (2.0 * freq_idx / head_dim))
        wave_len = 2.0 * math.pi / base_freq
        if wave_len > low_wave:
            freq_list.append(base_freq / ROPE_FACTOR)
        elif wave_len < high_wave:
            freq_list.append(base_freq)
        else:
            smooth = (ORIG_CONTEXT / wave_len - LOW_FACTOR) / (HIGH_FACTOR - LOW_FACTOR)
            freq_list.append((1.0 - smooth) * base_freq / ROPE_FACTOR + smooth * base_freq)
    return np.array(freq_list, dtype=np.float32)


def head_norm(values, gain):
    mean_sq = jnp.mean(values * values, axis=-1, keepdims=True)
    return values * lax.rsqrt(mean_sq + NORM_EPS) * gain


def softmax_rows(scores):
    top = jnp.max(scores, axis=-1, keepdims=True)
    weights = jnp.exp(scores - top)
    return (weights * (1.0 / jnp.sum(weights, axis=-1, keepdims=True))).astype(BF16)


def dot_nt(left, right):
    return lax.dot_general(left, right, (((1,), (1,)), ((), ())), preferred_element_type=F32)


def kernel(pos, tmask, freq, xg, ln1_a, ln2_a, ln1_b, ln2_b, qn, kn, hid, vis, wq_a, wk_a, wv_a, wo_a, wg_a, wu_a, wd_a, wq_b, wk_b, wv_b, wo_b, wg_b, wu_b, wd_b, out,
           ring, hbuf, xn, vbuf, gains, meta, cos_s, sin_s, fac, ks, vs, kb, vb, act, pall, psib, crcv, ssq, sprev, facc,
           wsem, lsem, ag_s, ag_r, mt_s, mt_r, vx_s, vx_r, vr_s, vr_r, vo_s, vo_r, ps_s, ps_r, cs_s, cs_r, hh_s, hh_r):
    me = lax.axis_index("tp")
    xi = lax.div(me, 2)
    co = lax.rem(me, 2)
    sib = xi * 2 + 1 - co
    cross = (1 - xi) * 2 + co
    diag = (1 - xi) * 2 + 1 - co

    def remote(src, dst, ssem, rsem, dev):
        return pltpu.make_async_remote_copy(src_ref=src, dst_ref=dst, send_sem=ssem, recv_sem=rsem, device_id={"tp": dev}, device_id_type=MESH)

    def spot(name, j):
        first, units, _ = SEG[name]
        return lax.rem(first + j * units, RING) * UNIT

    def panel_spot(name, j):
        return lax.rem(SEG[name][0] + j * KT, RING) * UNIT

    def put(weight, rows, col, at, sem, first=0):
        pltpu.make_async_copy(weight.at[pl.ds(first, rows), pl.ds(pl.multiple_of(col * HD, HD), HD)], ring.at[pl.ds(pl.multiple_of(at, HD), rows)], sem).start()

    def start_group(name, j):
        at = spot(name, j)
        base = SEMS[name]
        if name[:2] == "o_":
            for p in range(4):
                put(wo_a if name == "o_a" else wo_b, QW, j * 4 + p, at + p * QW, wsem.at[base + j])
        elif name == "gu_b":
            def pair(i, _):
                for p, w in enumerate((wg_b, wu_b)):
                    put(w, CW, i, at + (i * 2 + p) * CW, wsem.at[base + j], pl.multiple_of(j * CW, CW))
                return 0
            lax.fori_loop(0, FF // HD, pair, 0)
        elif name == "gu_a":
            put(wg_a, D, j, at, wsem.at[base + lax.rem(j, GU_SEMS)])
            put(wu_a, D, j, at + D, wsem.at[base + lax.rem(j, GU_SEMS)])
        elif name[:2] == "d_":
            for p in range(4):
                put(wd_a if name == "d_a" else wd_b, FF, j * 4 + p, at + p * 30 * UNIT, wsem.at[base + j])
        elif name == "q_b":
            put(wq_b, D, j, at, wsem.at[base + lax.div(j, 5)])
        elif name == "kv_b":
            for p, w in enumerate((wk_b, wk_b, wv_b, wv_b)):
                put(w, D, p % 2, at + p * D, wsem.at[base])
        else:
            for p in range(14):
                w = wq_a if p < 10 else (wk_a if p < 12 else wv_a)
                put(w, D, p if p < 10 else p % 2, at + p * D, wsem.at[base + p // 8])

    def ready(name, freed):
        first, units, count = SEG[name]
        if isinstance(freed, int):
            return min(max((freed + RING - first) // units, 0), count)
        return jnp.minimum(jnp.maximum(lax.div(freed + RING - first + 100 * units, units) - 100, 0), count)

    def refill(before, after, low, high, names=tuple(SEG)):
        for name in names:
            first, units, count = SEG[name]
            if first + units > high + RING or first + units * count <= low + RING:
                continue
            lo, hi = ready(name, before), ready(name, after)
            if isinstance(lo, int) and isinstance(hi, int) and lo >= hi:
                continue
            lax.fori_loop(lo, hi, lambda j, _, name=name: (start_group(name, j), 0)[1], 0)

    def landed(at, rows, sem):
        span = ring.at[pl.ds(pl.multiple_of(at, HD), rows)]
        pltpu.make_async_copy(span, span, sem).wait()

    def panel_set(spots, rows):
        return jnp.concatenate([ring[pl.ds(pl.multiple_of(at, HD), rows), :] for at in spots], axis=1)

    def panels(at, rows, pitch, count):
        return jnp.concatenate([ring[pl.ds(pl.multiple_of(at + p * pitch, HD), rows), :] for p in range(count)], axis=1)

    def mm(left, right):
        return jnp.dot(left, right, preferred_element_type=F32)

    def q_cols(i):
        start = (HEADS + i) * HD
        return pl.ds(start if isinstance(i, int) else pl.multiple_of(start, HD), HD)

    def q_group(g):
        return jnp.concatenate([act[:, q_cols(g * REP + i)] for i in range(REP)], axis=0)

    own_rows = pl.ds(pl.multiple_of(me * OWN, OWN), OWN)
    load_h = pltpu.make_async_copy(hid.at[0], hbuf.at[own_rows], lsem.at[0])
    load_h.start()
    load_v = pltpu.make_async_copy(vis.at[0], vbuf.at[me], lsem.at[1])
    load_v.start()
    barrier = pltpu.get_barrier_semaphore()
    for dev in (sib, cross, diag):
        pl.semaphore_signal(barrier, inc=1, device_id={"tp": dev}, device_id_type=MESH)
    for name in SEG:
        for j in range(ready(name, 0) if name == "qkv_a" else 0):
            start_group(name, j)
    row_i = lax.broadcasted_iota(jnp.int32, (OWN, HD), 0)
    lane_i = lax.broadcasted_iota(jnp.int32, (OWN, HD), 1)
    pos_row = jnp.concatenate([jnp.broadcast_to(pos[...].astype(F32), (OWN, OWN)), jnp.zeros((OWN, 96), F32)], axis=1)
    pos_col = jnp.sum(jnp.where(row_i == lane_i, pos_row, 0.0), axis=1, keepdims=True)
    own_meta = jnp.where(lane_i == 0, pos_col, 0.0)
    for j in range(TILES):
        tm_row = jnp.concatenate([jnp.broadcast_to(tmask[0, j:j + 1, :].astype(F32), (OWN, OWN)), jnp.zeros((OWN, 96), F32)], axis=1)
        tm_col = jnp.sum(jnp.where(row_i == lane_i, tm_row, 0.0), axis=1, keepdims=True)
        own_meta = jnp.where(lane_i == j + 1, tm_col, own_meta)
    meta[own_rows, :] = own_meta
    load_h.wait()
    pl.semaphore_wait(barrier, 3)

    def ag(kind, k):
        cols = pl.ds(k * (D // AGC), D // AGC)
        rows = pl.ds(pl.multiple_of((cross if kind == 2 else me) * OWN, OWN), OWN)
        ref = hbuf.at[rows, cols]
        return remote(ref, ref, ag_s, ag_r.at[(4, k, 5)[kind]], cross if kind == 1 else sib)

    def vown():
        return remote(vbuf.at[me], vbuf.at[me], vo_s, vo_r, sib)

    def vpiece(owner, k):
        return vbuf.at[owner, pl.ds(k // 2 * SUB, SUB), pl.ds(k % 2 * (D // 2), D // 2)]

    def vgroup(k):
        return 0 if k < VGROUP[1] else (1 if k < VGROUP[2] else 2)

    def vcross(k):
        return remote(vpiece(me, k), vpiece(me, k), vx_s, vx_r.at[vgroup(k)], cross)

    def vrelay(k):
        return remote(vpiece(cross, k), vpiece(cross, k), vr_s, vr_r.at[vgroup(k)], sib)

    def relay_vision(g):
        landed(0, (VGROUP[g + 1] - VGROUP[g]) * 320, vx_r.at[g])
        for k in range(VGROUP[g], VGROUP[g + 1]):
            vrelay(k).start()

    for k in range(AGC):
        ag(0, k).start()
    for k in range(AGC):
        ag(1, k).start()
    metas = [remote(meta.at[own_rows], meta.at[own_rows], mt_s, mt_r, dev) for dev in (sib, cross, diag)]
    for m in metas:
        m.start()
    load_v.wait()
    for k in range(5):
        vcross(k).start()

    for i, ln in enumerate((ln1_a, ln2_a, ln1_b, ln2_b)):
        for p in range(D // HD):
            gains[i:i + 1, p * HD:(p + 1) * HD] = ln[p:p + 1, :].astype(F32)
    q_gain = qn[...].astype(F32)
    k_gain = kn[...].astype(F32)

    def norm_rows(first, count, gain):
        def block(b, _):
            rows = pl.ds(pl.multiple_of(first + b * SUB, SUB), SUB)
            v = hbuf[rows, :].astype(F32)
            scale = lax.rsqrt(jnp.mean(v * v, axis=-1, keepdims=True) + NORM_EPS)
            xn[rows, :] = (v * scale * gains[gain:gain + 1, :]).astype(BF16)
            return 0
        lax.fori_loop(0, count // SUB, block, 0)

    norm_rows(me * OWN, OWN, 0)
    landed(0, OWN * KT, ag_r.at[4])
    norm_rows(sib * OWN, OWN, 0)
    landed(0, 3 * PAIR, mt_r)
    angles = meta[:, 0:1] * freq[...]
    cos_s[...] = jnp.cos(angles)
    lanes = lax.broadcasted_iota(jnp.int32, (TOK, HD), 1)
    sin_s[...] = jnp.where(lanes < HD // 2, -jnp.sin(angles), jnp.sin(angles))
    keep = jnp.max(jnp.where((lanes >= 1) & (lanes <= TILES), meta[...], 0.0), axis=1, keepdims=True)
    for i in range(2):
        fac[i] = jnp.where(keep > 0.0, jnp.tanh(jnp.full((TOK, HW), xg[i], F32)), 0.0)
    for k in range(AGC):
        ag(1, k).wait_recv()
        ag(2, k).start()
    refill(-RING, 0, 560 - RING, 0)
    norm_rows(cross * OWN, OWN, 0)

    landed(0, OWN * KT, ag_r.at[5])
    norm_rows(diag * OWN, OWN, 0)
    vown().start()

    def rope(v):
        return (v * cos_s[...] + pltpu.roll(v, HD // 2, 1) * sin_s[...]).astype(BF16)

    at = spot("qkv_a", 0)
    landed(at, 8 * D, wsem.at[0])
    landed(at + 8 * D, 6 * D, wsem.at[1])
    r = mm(xn[...], panels(at, D, D, 8))
    for i in range(8):
        act[:, q_cols(i)] = rope(r[:, i * HD:(i + 1) * HD])
    r = mm(xn[...], panels(at + 8 * D, D, D, 6))
    for i in range(2):
        act[:, q_cols(8 + i)] = rope(r[:, i * HD:(i + 1) * HD])
        ks[i] = rope(r[:, (2 + i) * HD:(3 + i) * HD])
        vs[i] = r[:, (4 + i) * HD:(5 + i) * HD].astype(BF16)
    refill(0, 560, 0, 560)

    causal = lax.rem(lax.broadcasted_iota(jnp.int32, (REP * TOK, TOK), 0), TOK) >= lax.broadcasted_iota(jnp.int32, (REP * TOK, TOK), 1)
    for g in range(GROUPS):
        scores = dot_nt(q_group(g), ks[g]) * (HD ** -0.5)
        mixed = mm(softmax_rows(jnp.where(causal, scores, MASK_VALUE)), vs[g]).astype(BF16)
        for i in range(REP):
            act[:, (g * REP + i) * HD:(g * REP + i + 1) * HD] = mixed[i * TOK:(i + 1) * TOK]

    def to_sib(n):
        return remote(pall.at[n, 1 - co], psib.at[n], ps_s, ps_r.at[n], sib)

    def to_cross(n, par, half):
        if half:
            rows = pl.ds(pl.multiple_of((1 - xi) * PAIR, PAIR), PAIR)
            return remote(pall.at[n, co, rows], crcv.at[par, n, rows], cs_s, cs_r.at[par, n], cross)
        return remote(pall.at[n, co], crcv.at[par, n], cs_s, cs_r.at[par, n], cross)

    def half_cols(n):
        return pl.ds(pl.multiple_of(n * CW + co * HW, HW), HW)

    def h_out(n):
        ref = hbuf.at[:, half_cols(n)]
        return remote(ref, ref, hh_s, hh_r.at[n], sib)

    def each(fn):
        lax.fori_loop(0, CH, lambda n, _: (fn(n), 0)[1], 0)

    def reduce_out(name, left, rows, pitch, par, half, early, lag, fill=None):
        first, units, _ = SEG[name]

        def pair_sum(n):
            to_sib(n).wait_recv()
            pall[n, co] = (pall[n, co].astype(F32) + psib[n].astype(F32)).astype(BF16)
            to_cross(n, par, half).start()

        def chunk(n):
            start = spot(name, n)
            landed(start, 4 * rows, wsem.at[SEMS[name] + n])
            part = mm(left[...], panels(start, rows, pitch, 4))
            part = part.astype(BF16)
            for k in range(2):
                if half:
                    blocks = [part[r:r + OWN, q:q + HW] for r in (OWN * k, PAIR + OWN * k) for q in (0, HW)]
                    pall[n, k] = jnp.concatenate(blocks, axis=0)
                else:
                    pall[n, k] = part[:, k * HW:(k + 1) * HW]
            to_sib(n).start()
            if fill is None:
                refill(first + n * units, first + (n + 1) * units, first, first + CH * units)
            else:
                fill(n)

            if early < lag:
                @pl.when(n == early)
                def _():
                    pair_sum(0)

            @pl.when(n >= (lag if early == lag else lag + 1))
            def _():
                pair_sum(n - lag)

        each(chunk)
        for n in range(CH - lag, CH):
            pair_sum(n)

    def finish(par, factor, gain):
        def squares(v):
            v = v.astype(F32)
            v = v * v
            ssq[...] += v[:, :HD] + v[:, HD:]

        def absorb(n):
            h_out(n).wait_recv()
            squares(hbuf[:, pl.ds(pl.multiple_of(n * CW + (1 - co) * HW, HW), HW)])

        def chunk(n):
            to_cross(n, par, False).wait_recv()
            total = pall[n, co].astype(F32) + crcv[par, n].astype(F32)
            if factor is not None:
                total = fac[factor] * total
            cols = half_cols(n)
            fresh = (hbuf[:, cols].astype(F32) + total).astype(BF16)
            hbuf[:, cols] = fresh
            h_out(n).start()
            squares(fresh)

            @pl.when(n >= 2)
            def _():
                absorb(n - 2)

        ssq[...] = jnp.zeros_like(ssq)
        each(chunk)
        absorb(CH - 2)
        absorb(CH - 1)
        ssq[...] = jnp.broadcast_to(lax.rsqrt(jnp.sum(ssq[...], axis=1, keepdims=True) * (1.0 / D) + NORM_EPS), (TOK, HD))

        def block(b, _):
            rows = pl.ds(pl.multiple_of(b * SUB, SUB), SUB)
            xn[rows, :] = (hbuf[rows, :].astype(F32) * ssq[rows, 0:1] * gains[gain:gain + 1, :]).astype(BF16)
            return 0

        lax.fori_loop(0, TOK // SUB, block, 0)

        for sem in (hh_s, ps_s, cs_s):
            landed(0, CH * 2 * TOK, sem)

    def gate_up(name):
        first = SEG[name][0]

        def pairs(j, count):
            spots = [panel_spot(name, j * 2 + p) for p in range(2 * count)]
            for p in range(count):
                landed(spots[p * 2], 2 * D, wsem.at[SEMS[name] + lax.rem(j + p, GU_SEMS)])
            part = mm(xn[...], panel_set(spots, D))
            for p in range(count):
                gate = part[:, p * HW:p * HW + HD]
                up = part[:, p * HW + HD:p * HW + HW]
                act[:, pl.ds(pl.multiple_of((j + p) * HD, HD), HD)] = (jax.nn.silu(gate) * up).astype(BF16)
            refill(first + j * 80, first + (j + count) * 80, first, first + 2160, ("gu_a", "d_a"))

        lax.fori_loop(0, 6, lambda i, _: (pairs(i * 4, 4), 0)[1], 0)
        pairs(jnp.int32(24), 3)

    landed(0, 3 * OWN * KT, ag_s)
    reduce_out("o_a", act.at[:, 0:HEADS * HD], QW, QW, 0, False, 2, 2)
    for k in range(5, 14):
        vcross(k).start()
    finish(0, None, 1)
    relay_vision(0)
    gate_up("gu_a")

    def fill_late(n):
        @pl.when(n == CH // 2)
        def _():
            refill(0, 3840, 0, 3840, ("q_b", "kv_b"))

    reduce_out("d_a", act, FF, 30 * UNIT, 1, False, 1, 2, fill_late)
    for k in range(14, VCH):
        vcross(k).start()

    kv_at = spot("kv_b", 0)

    def kv_rows(states, spots):
        part = mm(states, panels(kv_at, D, D, 4))
        done = 0
        for rows, count in spots:
            piece = part[done:done + count]
            for g in range(GROUPS):
                kb[g, rows, :] = head_norm(piece[:, g * HD:(g + 1) * HD], k_gain).astype(BF16)
                vb[g, rows, :] = piece[:, (2 + g) * HD:(3 + g) * HD].astype(BF16)
            done += count

    def block_rows(b, start, count):
        return pl.ds(pl.multiple_of(b * TOK + start, SUB), count)

    landed(kv_at, 4 * D, wsem.at[SEMS["kv_b"]])
    vown().wait_recv()

    def near(i, _):
        b = me + i * (sib - me)
        kv_rows(vbuf[b], [(block_rows(b, 0, TOK), TOK)])
        return 0

    def far(i, _):
        b = cross + i * (diag - cross)
        kv_rows(vbuf[b, 0:EARLY, :], [(block_rows(b, 0, EARLY), EARLY)])
        return 0

    lax.fori_loop(0, 2, near, 0)
    relay_vision(1)
    refill(0, 4320, 0, 4320, ("o_b", "gu_b"))
    for g in range(2):
        landed(0, (VGROUP[g + 1] - VGROUP[g]) * 320, vr_r.at[g])
    lax.fori_loop(0, 2, far, 0)
    finish(1, None, 2)
    sprev[...] = ssq[...]

    q_spots = [panel_spot("q_b", j) for j in range(HEADS)]
    for i in range(2):
        landed(q_spots[i * 5], 5 * D, wsem.at[SEMS["q_b"] + i])
    for g in range(GROUPS):
        if g == 1:
            relay_vision(2)
        r = mm(xn[...], panel_set(q_spots[g * REP:(g + 1) * REP], D))
        for i in range(REP):
            act[:, q_cols(g * REP + i)] = head_norm(r[:, i * HD:(i + 1) * HD], q_gain).astype(BF16)
    refill(4320, 4720, 4320, 4720)
    landed(0, (VGROUP[3] - VGROUP[2]) * 320, vr_r.at[2])
    rest = TOK - EARLY
    kv_rows(jnp.concatenate([vbuf[cross, EARLY:, :], vbuf[diag, EARLY:, :]], axis=0),
            [(block_rows(b, EARLY, rest), rest) for b in (cross, diag)])
    refill(4720, 4880, 4720, 4880)

    for i in range(HEADS):
        scores = dot_nt(act[:, q_cols(i)], kb[i // REP]) * (HD ** -0.5)
        facc[2 * i] = scores[:, :HW]
        facc[2 * i + 1] = scores[:, HW:]

    def soft(b, _):
        rows = pl.ds(pl.multiple_of(b * OWN, OWN), OWN)
        seen = [jnp.broadcast_to(meta[rows, j + 1:j + 2], (OWN, HD)) > 0.0 for j in range(TILES)]
        for i in range(HEADS):
            parts = [facc[2 * i + j // 2, rows, j % 2 * HD:(j % 2 + 1) * HD] for j in range(TILES)]
            weights = softmax_rows(jnp.concatenate([jnp.where(m, v, MASK_VALUE) for m, v in zip(seen, parts)], axis=1))
            pall[i, 0, rows] = weights[:, :HW]
            pall[i, 1, rows] = weights[:, HW:]
        return 0

    lax.fori_loop(0, TOK // OWN, soft, 0)
    for g in range(GROUPS):
        heads = range(g * REP, (g + 1) * REP)
        mixed = sum(mm(jnp.concatenate([pall[i, p] for i in heads], axis=0), vb[g, p * HW:(p + 1) * HW, :]) for p in range(2)).astype(BF16)
        for n, i in enumerate(heads):
            act[:, i * HD:(i + 1) * HD] = mixed[n * TOK:(n + 1) * TOK]

    reduce_out("o_b", act.at[:, 0:HEADS * HD], QW, QW, 0, False, 2, 3)
    def finish_gate_up():
        first = SEG["gu_b"][0]

        def take(v, cols):
            v = v.astype(F32)
            sq = v * v
            ssq[...] += sq[:, :HD] + sq[:, HD:]
            xn[:, cols] = (v * sprev[:, 0:1] * gains[3:4, cols]).astype(BF16)

        def absorb(n):
            h_out(n).wait_recv()
            cols = pl.ds(pl.multiple_of(n * CW + (1 - co) * HW, HW), HW)
            take(hbuf[:, cols], cols)

        def own(n):
            to_cross(n, 0, False).wait_recv()
            cols = half_cols(n)
            total = fac[0] * (pall[n, co].astype(F32) + crcv[0, n].astype(F32))
            fresh = (hbuf[:, cols].astype(F32) + total).astype(BF16)
            hbuf[:, cols] = fresh
            h_out(n).start()
            take(fresh, cols)

        def products(n, store):
            at = spot("gu_b", n)
            left = xn[:, pl.ds(pl.multiple_of(n * CW, CW), CW)]
            for p in range(0, FF // HD, 4):
                count = min(4, FF // HD - p)
                part = mm(left, panel_set([at + (p * 2 + j) * CW for j in range(2 * count)], CW))
                for q in range(count):
                    store(p + q, part[:, q * HW:(q + 1) * HW])

        def arrive(n):
            landed(spot("gu_b", n), FF // PAIR * CW, wsem.at[SEMS["gu_b"] + n])

        def add(p, part):
            facc[p] += part

        def middle(n):
            absorb(n)
            arrive(n)
            products(n, add)

            refill(first + n * 240, first + (n + 1) * 240, first, first + 2160)

        def step(n):
            own(n)

            @pl.when(n >= 1)
            def _():
                middle(n - 1)

        ssq[...] = jnp.zeros_like(ssq)
        facc[...] = jnp.zeros_like(facc)
        each(step)
        last_n = jnp.int32(CH - 1)
        absorb(last_n)
        arrive(last_n)
        scale = lax.rsqrt(jnp.sum(ssq[...], axis=1, keepdims=True) * (1.0 / D) + NORM_EPS)
        ssq[...] = jnp.broadcast_to(scale, (TOK, HD)) / sprev[...]

        def activate(p, part):
            both = facc[p] + part
            act[:, p * HD:(p + 1) * HD] = (jax.nn.silu(both[:, :HD] * ssq[...]) * (both[:, HD:] * ssq[...])).astype(BF16)

        products(last_n, activate)
        refill(first + 2160, first + 2400, first + 2160, first + 2400)

        for sem in (hh_s, ps_s, cs_s):
            landed(0, CH * 2 * TOK, sem)

    finish_gate_up()
    vown().wait_send()
    landed(0, TOK * KT, vx_s)
    landed(0, TOK * KT, vr_s)
    reduce_out("d_b", act, FF, 30 * UNIT, 1, True, 2, 2)

    chip_rows = pl.ds(pl.multiple_of(xi * PAIR, PAIR), PAIR)

    def last(n):
        to_cross(n, 1, True).wait_recv()
        total = pall[n, co, chip_rows].astype(F32) + crcv[1, n, chip_rows].astype(F32)
        for q in range(2):
            cols = pl.ds(pl.multiple_of(n * CW + q * HW, HW), HW)
            xn[0:OWN, cols] = (hbuf[own_rows, cols].astype(F32) + fac[1, own_rows] * total[q * OWN:(q + 1) * OWN]).astype(BF16)
        cols = pl.ds(pl.multiple_of(n * CW, CW), CW)
        pltpu.make_async_copy(xn.at[0:OWN, cols], out.at[0, :, cols], lsem.at[2]).start()

    each(last)
    landed(0, CH * 2 * TOK, ps_s)
    landed(0, CH * TOK, cs_s)
    landed(0, 3 * PAIR, mt_s)
    landed(0, OWN * KT, lsem.at[2])


def solution(mesh):
    act_spec = P('dp', 'tp', None)
    col_spec = P(None, 'tp')
    row_spec = P('tp', None)
    layer_a = (P(), col_spec, col_spec, col_spec, row_spec, P(), col_spec, col_spec, row_spec)
    layer_b = (P(), col_spec, P(), col_spec, col_spec, P(), row_spec, P(), col_spec, col_spec, row_spec, P())
    in_specs = (act_spec, act_spec, P('dp', 'tp'), act_spec) + layer_a + layer_b

    def body(hidden, vision, positions, tile_mask, ln1_a, wq_a, wk_a, wv_a, wo_a, ln2_a, wg_a, wu_a, wd_a, ln1_b, wq_b, q_norm, wk_b, wv_b, k_norm, wo_b, ln2_b, wg_b, wu_b, wd_b, xgates):
        freq = rope_table(HD)
        freq = jnp.asarray(np.concatenate([freq, freq])[None, :])
        lns = [g.reshape(D // HD, HD) for g in (ln1_a, ln2_a, ln1_b, ln2_b)]
        heads = [g.reshape(1, HD) for g in (q_norm, k_norm)]
        vmem = pl.BlockSpec(memory_space=pltpu.VMEM)
        hbm = pl.BlockSpec(memory_space=pl.ANY)
        dma = pltpu.SemaphoreType.DMA
        return pl.pallas_call(
            kernel,
            out_shape=jax.ShapeDtypeStruct((1, OWN, D), BF16),
            in_specs=[vmem] * 3 + [pl.BlockSpec(memory_space=pltpu.SMEM)] + [vmem] * 6 + [hbm] * SUB,
            out_specs=hbm,
            scratch_shapes=[
                pltpu.VMEM((RING * UNIT, HD), BF16),
                pltpu.VMEM((TOK, D), BF16),
                pltpu.VMEM((TOK, D), BF16),
                pltpu.VMEM((4, TOK, D), BF16),
                pltpu.VMEM((4, D), F32),
                pltpu.VMEM((TOK, HD), F32),
                pltpu.VMEM((TOK, HD), F32),
                pltpu.VMEM((TOK, HD), F32),
                pltpu.VMEM((2, TOK, HW), F32),
                pltpu.VMEM((GROUPS, TOK, HD), BF16),
                pltpu.VMEM((GROUPS, TOK, HD), BF16),
                pltpu.VMEM((GROUPS, 4 * TOK, HD), BF16),
                pltpu.VMEM((GROUPS, 4 * TOK, HD), BF16),
                pltpu.VMEM((TOK, FF), BF16),
                pltpu.VMEM((CH, 2, TOK, HW), BF16),
                pltpu.VMEM((CH, TOK, HW), BF16),
                pltpu.VMEM((2, CH, TOK, HW), BF16),
                pltpu.VMEM((TOK, HD), F32),
                pltpu.VMEM((TOK, HD), F32),
                pltpu.VMEM((FF // HD, TOK, HW), F32),
                dma((NSEM,)), dma((3,)),
                dma(()), dma((6,)),
                dma(()), dma(()),
                dma(()), dma((3,)),
                dma(()), dma((3,)),
                dma(()), dma(()),
                dma(()), dma((CH,)),
                dma(()), dma((2, CH)),
                dma(()), dma((CH,)),
            ],
            compiler_params=pltpu.CompilerParams(collective_id=0, has_side_effects=True, vmem_limit_bytes=67043328),
        )(positions, jnp.swapaxes(tile_mask, 1, 2), freq, xgates, *lns, *heads, hidden, vision, wq_a, wk_a, wv_a, wo_a, wg_a, wu_a, wd_a, wq_b, wk_b, wv_b, wo_b, wg_b, wu_b, wd_b)

    return jax.shard_map(body, mesh=mesh, in_specs=in_specs, out_specs=act_spec, check_vma=False)
```

time: 148 us -> 121 us (0.82)
  Pallas kernels: 136 us -> 119 us
  local copies, waits for them, and re-layouts: 9.74 us -> 1.72 us
    pallas_call x1, Pallas kernels: 136 us -> 119 us  [body(): pl.pallas_call(kernel, out_shape=jax.ShapeDtypeStruct((1, OWN, D), BF16),...]
    another operation x7 -> x0, local copies, waits for them, and re-layouts: 5.41 us -> none  [the longest x4 2.87 us: body(): gains = jnp.stack([ln1_a, ln2_a, ln1_b, ln2_b]).astype(F32)]
    unnamed x2 -> x1, local copies, waits for them, and re-layouts: 3.08 us -> 1.72 us
where the time goes in v2:
time: 121 us
  Pallas kernels  119 us (98%)
  local copies, waits for them, and re-layouts  1.72 us (1%)
    pallas_call x1, Pallas kernels, body(): pl.pallas_call(kernel, out_shape=jax.ShapeDtypeStruct((1, OWN, D), BF16),...  119 us

profile of v2, /device:TPU:0, one launch (start us, length us, event | category | flops | bytes accessed | tf_op | source)
XLA Modules:
  0.0 120.5 jit_solution(15992777717352657883)
XLA Ops:
  0.0 118.8 %shard_map.244 = bf16[1,32,5120]{2,1,0:T(8,128)(2,1)} custom-call(s32[1,32]{1,0:T(1,128)} %pos.1, s32[1,4,32]{2,1,0:T(4,128)} %bitcast.11, f32[1,128]{1,0:T(1,128)} %constant.2.clone.freq, f32[2]{0:T(128)} %xg.1, bf16[40,128]{1,0:T(8,128)(2,1)} %bitcast.7, bf16[40,128]{1,0:T(8,128)(2,1)} %bitcast.8, bf16[40,128]{1,0:T(8,128)(2,1)} %bitcast.9, ...), custom_call_target="tpu_custom_call" | custom-call | tf_op jit(solution)/shard_map/pallas_call | solution.py:619
  118.8 1.7 %copy.28 = bf16[1,32,5120]{2,1,0:T(8,128)(2,1)} copy(bf16[1,32,5120]{2,1,0:T(8,128)(2,1)} %shard_map.244) | data formatting | bytes 655360

commit v3 on v2

--- a/solution.py
+++ b/solution.py
@@ -120,11 +120,12 @@
             for p in range(4):
                 put(wo_a if name == "o_a" else wo_b, QW, j * 4 + p, at + p * QW, wsem.at[base + j])
         elif name == "gu_b":
-            def pair(i, _):
-                for p, w in enumerate((wg_b, wu_b)):
-                    put(w, CW, i, at + (i * 2 + p) * CW, wsem.at[base + j], pl.multiple_of(j * CW, CW))
+            def pairs(i, _):
+                for q in range(9):
+                    for p, w in enumerate((wg_b, wu_b)):
+                        put(w, CW, i * 9 + q, at + (i * 18 + q * 2 + p) * CW, wsem.at[base + j], pl.multiple_of(j * CW, CW))
                 return 0
-            lax.fori_loop(0, FF // HD, pair, 0)
+            lax.fori_loop(0, FF // HD // 9, pairs, 0)
         elif name == "gu_a":
             put(wg_a, D, j, at, wsem.at[base + lax.rem(j, GU_SEMS)])
             put(wu_a, D, j, at + D, wsem.at[base + lax.rem(j, GU_SEMS)])
@@ -157,6 +158,9 @@
                 continue
             lax.fori_loop(lo, hi, lambda j, _, name=name: (start_group(name, j), 0)[1], 0)
 
+    def start_all(name):
+        lax.fori_loop(0, SEG[name][2], lambda j, _: (start_group(name, j), 0)[1], 0)
+
     def landed(at, rows, sem):
         span = ring.at[pl.ds(pl.multiple_of(at, HD), rows)]
         pltpu.make_async_copy(span, span, sem).wait()
@@ -181,13 +185,9 @@
     load_h = pltpu.make_async_copy(hid.at[0], hbuf.at[own_rows], lsem.at[0])
     load_h.start()
     load_v = pltpu.make_async_copy(vis.at[0], vbuf.at[me], lsem.at[1])
-    load_v.start()
     barrier = pltpu.get_barrier_semaphore()
     for dev in (sib, cross, diag):
         pl.semaphore_signal(barrier, inc=1, device_id={"tp": dev}, device_id_type=MESH)
-    for name in SEG:
-        for j in range(ready(name, 0) if name == "qkv_a" else 0):
-            start_group(name, j)
     row_i = lax.broadcasted_iota(jnp.int32, (OWN, HD), 0)
     lane_i = lax.broadcasted_iota(jnp.int32, (OWN, HD), 1)
     pos_row = jnp.concatenate([jnp.broadcast_to(pos[...].astype(F32), (OWN, OWN)), jnp.zeros((OWN, 96), F32)], axis=1)
@@ -234,9 +234,8 @@
     metas = [remote(meta.at[own_rows], meta.at[own_rows], mt_s, mt_r, dev) for dev in (sib, cross, diag)]
     for m in metas:
         m.start()
-    load_v.wait()
-    for k in range(5):
-        vcross(k).start()
+    load_v.start()
+    start_group("qkv_a", 0)
 
     for i, ln in enumerate((ln1_a, ln2_a, ln1_b, ln2_b)):
         for p in range(D // HD):
@@ -267,6 +266,10 @@
     for k in range(AGC):
         ag(1, k).wait_recv()
         ag(2, k).start()
+        if k == AGC - 2:
+            load_v.wait()
+            for j in range(VGROUP[1]):
+                vcross(j).start()
     refill(-RING, 0, 560 - RING, 0)
     norm_rows(cross * OWN, OWN, 0)
 
@@ -375,14 +378,9 @@
             h_out(n).start()
             squares(fresh)
 
-            @pl.when(n >= 2)
-            def _():
-                absorb(n - 2)
-
         ssq[...] = jnp.zeros_like(ssq)
         each(chunk)
-        absorb(CH - 2)
-        absorb(CH - 1)
+        each(absorb)
         ssq[...] = jnp.broadcast_to(lax.rsqrt(jnp.sum(ssq[...], axis=1, keepdims=True) * (1.0 / D) + NORM_EPS), (TOK, HD))
 
         def block(b, _):
@@ -421,9 +419,10 @@
     gate_up("gu_a")
 
     def fill_late(n):
-        @pl.when(n == CH // 2)
-        def _():
-            refill(0, 3840, 0, 3840, ("q_b", "kv_b"))
+        for when, name in ((2, "kv_b"), (CH // 2, "q_b")):
+            @pl.when(n == when)
+            def _(name=name):
+                start_all(name)
 
     reduce_out("d_a", act, FF, 30 * UNIT, 1, False, 1, 2, fill_late)
     for k in range(14, VCH):

time: 121 us -> 116 us (0.959)
  Pallas kernels: 119 us -> 115 us
    pallas_call x1, Pallas kernels: 119 us -> 115 us  [body(): pl.pallas_call(kernel, out_shape=jax.ShapeDtypeStruct((1, OWN, D), BF16),...]
where the time goes in v3:
time: 116 us
  Pallas kernels  115 us (99%)
  local copies, waits for them, and re-layouts  1.72 us (1%)
    pallas_call x1, Pallas kernels, body(): pl.pallas_call(kernel, out_shape=jax.ShapeDtypeStruct((1, OWN, D), BF16),...  115 us

profile of v3, /device:TPU:0, one launch (start us, length us, event | category | flops | bytes accessed | tf_op | source)
XLA Modules:
  0.0 116.2 jit_solution(8246814325150603605)
XLA Ops:
  0.0 114.5 %shard_map.244 = bf16[1,32,5120]{2,1,0:T(8,128)(2,1)} custom-call(s32[1,32]{1,0:T(1,128)} %pos.1, s32[1,4,32]{2,1,0:T(4,128)} %bitcast.11, f32[1,128]{1,0:T(1,128)} %constant.2.clone.freq, f32[2]{0:T(128)} %xg.1, bf16[40,128]{1,0:T(8,128)(2,1)} %bitcast.7, bf16[40,128]{1,0:T(8,128)(2,1)} %bitcast.8, bf16[40,128]{1,0:T(8,128)(2,1)} %bitcast.9, ...), custom_call_target="tpu_custom_call" | custom-call | tf_op jit(solution)/shard_map/pallas_call | solution.py:618
  114.5 1.7 %copy.28 = bf16[1,32,5120]{2,1,0:T(8,128)(2,1)} copy(bf16[1,32,5120]{2,1,0:T(8,128)(2,1)} %shard_map.244) | data formatting | bytes 655360

commit v4 on v3

--- a/solution.py
+++ b/solution.py
@@ -39,7 +39,7 @@
 RING = 1440
 AGC = 4
 VCH = 16
-VGROUP = (0, 5, 14, 16)
+VGROUP = (0, 4, 14, 16)
 EARLY = 112
 
 SEG = {
@@ -412,7 +412,7 @@
 
     landed(0, 3 * OWN * KT, ag_s)
     reduce_out("o_a", act.at[:, 0:HEADS * HD], QW, QW, 0, False, 2, 2)
-    for k in range(5, 14):
+    for k in range(VGROUP[1], VGROUP[2]):
         vcross(k).start()
     finish(0, None, 1)
     relay_vision(0)

time: 116 us -> 115 us (level)
  Pallas kernels: 115 us -> 113 us
    pallas_call x1, Pallas kernels: 115 us -> 113 us  [body(): pl.pallas_call(kernel, out_shape=jax.ShapeDtypeStruct((1, OWN, D), BF16),...]
where the time goes in v4:
time: 115 us; the launch traced here: 114 us
  Pallas kernels  113 us (98%)
  local copies, waits for them, and re-layouts  1.72 us (1%)
    pallas_call x1, Pallas kernels, body(): pl.pallas_call(kernel, out_shape=jax.ShapeDtypeStruct((1, OWN, D), BF16),...  113 us

profile of v4, /device:TPU:0, one launch (start us, length us, event | category | flops | bytes accessed | tf_op | source)
XLA Modules:
  0.0 114.3 jit_solution(4408072308391426133)
XLA Ops:
  0.0 112.6 %shard_map.244 = bf16[1,32,5120]{2,1,0:T(8,128)(2,1)} custom-call(s32[1,32]{1,0:T(1,128)} %pos.1, s32[1,4,32]{2,1,0:T(4,128)} %bitcast.11, f32[1,128]{1,0:T(1,128)} %constant.2.clone.freq, f32[2]{0:T(128)} %xg.1, bf16[40,128]{1,0:T(8,128)(2,1)} %bitcast.7, bf16[40,128]{1,0:T(8,128)(2,1)} %bitcast.8, bf16[40,128]{1,0:T(8,128)(2,1)} %bitcast.9, ...), custom_call_target="tpu_custom_call" | custom-call | tf_op jit(solution)/shard_map/pallas_call | solution.py:618
  112.6 1.7 %copy.28 = bf16[1,32,5120]{2,1,0:T(8,128)(2,1)} copy(bf16[1,32,5120]{2,1,0:T(8,128)(2,1)} %shard_map.244) | data formatting | bytes 655360
